TPU v7x, 128 devices: a whole 4x4x4 slice. The times are simulated.
128 devices in a mesh: mom: 8 (over x_lo, y), en: 16 (over z, x_hi, core).
Axes of the slice: x: 4 (x_hi: 2, x_lo: 2; x = x_hi * 2 + x_lo), y: 4, z: 4, core: 2. Of those that a mesh axis runs over, the one named last changes fastest.
Arguments:
- green_blocks: float32 [24, 16, 2, 512, 512], P('mom', 'en'), may hold values from -6 to 6
- transfer_index: int32 [24, 24], P('mom'), may hold values from 0 to 8
- photon_shift: int32 [24], P('mom'), may hold values from 1 to 2
- photon_occupancy: float32 [1], replicated, may hold values from 0.3 to 3
- coupling: bfloat16 [9, 512, 512], replicated, may hold values from -0.25 to 0.25
Outputs:
- self_energy: float32 [24, 16, 2, 512, 512], P('mom', 'en')
All inputs are finite; a program needn't handle non-finite values.
Results may differ from a plain program's by a relative error of at most 0.0057.
Values may be sent and summed in bfloat16 or wider, within the bound.
A program may use at most 192 MiB of HBM per device.

v0:
```python
import functools

import jax
import jax.numpy as jnp
from jax import lax
from jax.experimental import pallas as pl
from jax.experimental.pallas import tpu as pltpu
from jax.sharding import PartitionSpec as P

MESH = pl.DeviceIdType.MESH
BF = jnp.bfloat16
F32 = jnp.float32

NX, NY, NZ = 2, 4, 4
ROWS = 32
SUB = 2
RELAYED = ("b1", "b3", "a1", "a3", "r1", "r3", "z", "do", "ds", "yp", "ym", "qp", "qm")


def kernel(n, nq, own_k, perm, ends, weight, green, coupling, out,
           stage, a, own, far, rp, rc, po, ps, whole, cmat, cst, block, prefix, bins, right, obf, orecv,
           load_sem, cload_sem, send_sem, recv_sem, osend_sem, orecv_sem, store_sem):
    chunks = n // ROWS
    half = ROWS // 2
    height = ROWS * SUB
    blocks = chunks // SUB
    pair_k = 2 * own_k
    every_k = NY * pair_k
    mom, en = lax.axis_index("mom"), lax.axis_index("en")
    xl, y = mom // NY, mom % NY
    z, xh, core = en // 4, (en // 2) % 2, en % 2
    part = xl
    mine, other = xl * own_k, (1 - xl) * own_k
    up, down = (y + 1) % NY, (y + NY - 1) % NY

    def place(axl, ay, az, axh, acore):
        return (axl * NY + ay, (az * 2 + axh) * 2 + acore)

    pair = place(1 - xl, y, z, xh, core)
    cross = place(1 - xl, y, z, 1 - xh, core)
    z_to = place(xl, y, (z + 1 + 2 * xh) % NZ, xh, core)
    z_from = place(xl, y, (z + 3 + 2 * xh) % NZ, xh, core)
    twin = place(xl, y, z, xh, 1 - core)
    y_up = place(xl, up, z, xh, core)
    y_down = place(xl, down, z, xh, core)
    side = (core + xh) % 2

    kinds = {name: i for i, name in enumerate(RELAYED)}

    def remote(name, r, src, dst, device):
        i = kinds[name]
        return pltpu.make_async_remote_copy(
            src_ref=src, dst_ref=dst, send_sem=send_sem.at[i], recv_sem=recv_sem.at[i, r],
            device_id=device, device_id_type=MESH)

    def first(r):
        return own.at[r, pl.ds(mine, own_k), pl.ds(0, half)]

    def second(r):
        return own.at[r, pl.ds(mine, own_k), pl.ds(half, half)]

    def copy(name, r):
        if name == "b1":
            return remote(name, r, first(r), rp.at[r], pair)
        if name == "b3":
            return remote(name, r, second(r), rc.at[r], cross)
        if name == "a1":
            return remote(name, r, a.at[r], own.at[r, pl.ds(mine, own_k)], pair)
        if name == "a3":
            return remote(name, r, a.at[r], far.at[0, r, pl.ds(mine, own_k)], cross)
        if name == "r3":
            return remote(name, r, rp.at[r], far.at[0, r, pl.ds(other, own_k), pl.ds(0, half)], cross)
        if name == "r1":
            return remote(name, r, rc.at[r], far.at[0, r, pl.ds(other, own_k), pl.ds(half, half)], pair)
        if name == "z":
            return remote(name, r, far.at[0, r], far.at[1, r], z_to)
        if name == "do":
            return remote(name, r, own.at[r], po.at[r], twin)
        if name == "ds":
            return remote(name, r, far.at[side, r], ps.at[r], twin)
        here = whole.at[r, pl.ds(y * pair_k, pair_k)]
        if name == "yp":
            return remote(name, r, here, here, y_up)
        if name == "ym":
            return remote(name, r, here, here, y_down)
        if name == "qp":
            got = whole.at[r, pl.ds(down * pair_k, pair_k), pl.ds(0, half)]
            return remote(name, r, got, got, y_up)
        got = whole.at[r, pl.ds(up * pair_k, pair_k), pl.ds(half, half)]
        return remote(name, r, got, got, y_down)

    def load(r):
        return pltpu.make_async_copy(
            green.at[:, 0, :, pl.ds(r * ROWS, ROWS)], stage.at[:, :, pl.ds(r * ROWS, ROWS)], load_sem.at[r])

    def convert(r):
        rows = pl.ds(r * ROWS, ROWS)
        for j in range(own_k):
            a[r, j] = stage[j, 1 - part, rows].astype(BF)
            own[r, mine + j] = stage[j, part, rows].astype(BF)

    pl.loop(0, chunks)(lambda r: load(r).start())
    cload = pltpu.make_async_copy(coupling, cmat, cload_sem)
    cload.start()
    barrier = pltpu.get_barrier_semaphore()
    for device in (pair, cross, z_to, z_from, twin, y_up, y_down):
        pl.semaphore_signal(barrier, inc=1, device_id=device, device_id_type=MESH)

    @pl.loop(0, chunks)
    def _(r):
        load(r).wait()
        convert(r)

    pl.semaphore_wait(barrier, 7)

    def mix(r):
        for i in range(pair_k):
            total = weight[i, 0] * po[r, i].astype(F32)
            total += weight[i, 1] * ps[r, i].astype(F32)
            total += weight[i, 2] * far[0, r, i].astype(F32)
            total += weight[i, 3] * far[1, r, i].astype(F32)
            whole[r, y * pair_k + i] = total.astype(BF)

    def classes(b):
        @pl.loop(0, every_k)
        def _(s):
            for u in range(SUB):
                block[s, u * ROWS:(u + 1) * ROWS] = whole[b * SUB + u, s]

        tiles = height // 16

        @pl.loop(0, pair_k * tiles)
        def _(i):
            k, tile = i // tiles, i % tiles
            rows = pl.ds(pl.multiple_of(tile * 16, 16), 16)
            total = jnp.zeros((16, n), F32)
            for j in range(every_k):
                total += block[perm[k, j], rows].astype(F32)
                prefix[j + 1] = total
            low = prefix[ends[k, 0]]
            to = pl.ds(pl.multiple_of(i * 16, 16), 16)
            for q in range(nq):
                high = prefix[ends[k, q + 1]]
                bins[q, to] = (high - low).astype(BF)
                low = high

        @pl.loop(0, nq)
        def _(q):
            product = lax.dot_general(
                bins[q], cmat[q], (((1,), (1,)), ((), ())), preferred_element_type=F32).astype(BF)
            at = pl.ds(pl.multiple_of(q * height, height), height)
            for k in range(pair_k):
                right[k, at] = product[k * height:(k + 1) * height]

    def osend(j):
        return pltpu.make_async_remote_copy(
            src_ref=obf.at[j], dst_ref=orecv.at[j], send_sem=osend_sem.at[j], recv_sem=orecv_sem.at[j],
            device_id=pair, device_id_type=MESH)

    total_of = stage

    def close(b):
        @pl.loop(0, pair_k)
        def _(i):
            k = (other + i) % pair_k
            term = jnp.dot(cst[b], right[k], preferred_element_type=F32)

            @pl.when(b == 0)
            def _():
                total_of[k // 2, k % 2] = term

            @pl.when(b > 0)
            def _():
                total_of[k // 2, k % 2] += term

            @pl.when((b == blocks - 1) & (i < own_k))
            def _():
                obf[i] = (total_of[k // 2, k % 2] / every_k).astype(BF)

            @pl.when((b == blocks - 1) & (i >= 1) & (i < own_k + 1))
            def _():
                osend(i - 1).start()

    def when(ok, names, what):
        pl.when(ok)(lambda: what())

    def within(r):
        return (r >= 0) & (r < chunks)

    @pl.loop(0, chunks + 6)
    def _(t):
        @pl.when(within(t))
        def _():
            for name in ("b1", "b3", "a1", "a3"):
                copy(name, t).start()
            copy("b1", t).wait_recv()
            copy("r3", t).start()
            copy("b3", t).wait_recv()
            copy("r1", t).start()

        @pl.when(t == 0)
        def _():
            cload.wait()
            prefix[0] = jnp.zeros((16, n), F32)
            right[:, nq * height:] = jnp.zeros((pair_k, right.shape[1] - nq * height, n), BF)
            lane = lax.broadcasted_iota(jnp.int32, (n, 128), 1) < height

            @pl.loop(0, (nq + 1) // 2)
            def _(h):
                for d in range(n // 128):
                    lhs = cmat[2 * h, :, d * 128:(d + 1) * 128].astype(F32)
                    rhs = cmat[jnp.minimum(2 * h + 1, nq - 1), :, d * 128:(d + 1) * 128].astype(F32)
                    rhs = jnp.where(2 * h + 1 < nq, rhs, jnp.zeros_like(rhs))
                    to = pl.ds(pl.multiple_of(h * 128, 128), 128)
                    cst[2 * d, :, to] = jnp.where(lane, lhs, pltpu.roll(rhs, height, 1)).astype(BF)
                    cst[2 * d + 1, :, to] = jnp.where(lane, pltpu.roll(lhs, height, 1), rhs).astype(BF)

        @pl.when(within(t - 3))
        def _():
            r = t - 3
            copy("do", r).wait_recv()
            copy("ds", r).wait_recv()
            mix(r)

        @pl.when(within(t - 1))
        def _():
            r = t - 1
            copy("a3", r).wait_recv()
            copy("r3", r).wait_recv()
            copy("r1", r).wait_recv()
            copy("z", r).start()
            copy("a1", r).wait_recv()
            copy("do", r).start()

        @pl.when(within(t - 2))
        def _():
            r = t - 2
            copy("z", r).wait_recv()
            copy("ds", r).start()

        @pl.when(within(t - 3))
        def _():
            copy("yp", t - 3).start()
            copy("ym", t - 3).start()

        @pl.when(within(t - 4))
        def _():
            r = t - 4
            copy("yp", r).wait_recv()
            copy("qp", r).start()
            copy("ym", r).wait_recv()
            copy("qm", r).start()

        @pl.when(within(t - 5))
        def _():
            r = t - 5
            copy("qp", r).wait_recv()
            copy("qm", r).wait_recv()

            @pl.when(r % SUB == SUB - 1)
            def _():
                classes(r // SUB)

        @pl.when(within(t - 6) & ((t - 6) % SUB == SUB - 1))
        def _():
            close((t - 6) // SUB)

    for name, ref in (("b1", rp), ("b3", rc), ("a1", a), ("a3", a), ("r1", rc), ("r3", rp), ("z", far.at[0]),
                      ("do", own), ("ds", ps), ("yp", own), ("ym", own), ("qp", a), ("qm", a)):
        pltpu.make_async_copy(ref, ref, send_sem.at[kinds[name]]).wait()

    def store(j, p, k):
        return pltpu.make_async_copy(total_of.at[k // 2, k % 2], out.at[j, 0, p], store_sem.at[j, p])

    for j in range(own_k):
        k = mine + j
        total_of[k // 2, k % 2] = total_of[k // 2, k % 2] / every_k
        store(j, part, k).start()
    for j in range(own_k):
        k = other + j
        osend(j).wait_recv()
        total_of[k // 2, k % 2] = orecv[j].astype(F32)
        store(j, 1 - part, k).start()
    for j in range(own_k):
        osend(j).wait_send()
        store(j, part, mine + j).wait()
        store(j, 1 - part, other + j).wait()


def body(green_blocks, transfer_index, photon_shift, photon_occupancy, coupling):
    own_k, n = green_blocks.shape[0], green_blocks.shape[3]
    momenta, nq = transfer_index.shape[1], coupling.shape[0]
    pair_k = 2 * own_k
    chunks, height = n // ROWS, ROWS * SUB
    deep = (nq + 1) // 2 * 2 * height
    mom, en = lax.axis_index("mom"), lax.axis_index("en")
    count = lax.axis_size("en")
    xl = mom // NY
    xh, core = (en // 2) % 2, en % 2

    packed = jnp.concatenate([transfer_index, photon_shift[:, None]], axis=1)
    others = lax.ppermute(packed, "mom", [(i, (i + NY) % (NX * NY)) for i in range(NX * NY)])
    both = jnp.where(xl == 0, jnp.stack([packed, others]), jnp.stack([others, packed]))
    both = both.reshape(pair_k, momenta + 1)
    shift = both[:, momenta]
    table = both[:, :momenta].reshape(pair_k, NX, NY, own_k).transpose(0, 2, 1, 3).reshape(pair_k, momenta)
    slot = jnp.arange(momenta, dtype=jnp.int32)
    key = table * 64 + slot
    rank = jnp.sum((key[:, None, :] < key[:, :, None]).astype(jnp.int32), axis=2)
    perm = jnp.sum(jnp.where(rank[:, :, None] == slot, slot[None, :, None], 0), axis=1)
    ends = jnp.sum((table[:, None, :] < jnp.arange(nq + 1, dtype=jnp.int32)[None, :, None]).astype(jnp.int32), axis=2)
    occupy = photon_occupancy[0]
    near = shift == 1
    zero = jnp.zeros_like(occupy)
    below1 = jnp.where(near & (en >= 1), occupy, zero)
    above1 = jnp.where(near & (en + 1 < count), occupy + 1.0, zero)
    below2 = jnp.where(~near & (en >= 2), occupy, zero)
    above2 = jnp.where(~near & (en + 2 < count), occupy + 1.0, zero)
    weight = jnp.stack([
        jnp.where(core == 0, above1, below1), jnp.where(core == 0, below1, above1),
        jnp.where(xh == 0, above2, below2), jnp.where(xh == 0, below2, above2)], axis=1)

    smem = pl.BlockSpec(memory_space=pltpu.SMEM)
    hbm = pl.BlockSpec(memory_space=pl.ANY)
    dma = pltpu.SemaphoreType.DMA
    return pl.pallas_call(
        functools.partial(kernel, n, nq, own_k),
        out_shape=jax.ShapeDtypeStruct(green_blocks.shape, F32),
        in_specs=[smem, smem, smem, hbm, hbm],
        out_specs=hbm,
        scratch_shapes=[
            pltpu.VMEM((own_k, 2, n, n), F32),
            pltpu.VMEM((chunks, own_k, ROWS, n), BF),
            pltpu.VMEM((chunks, pair_k, ROWS, n), BF),
            pltpu.VMEM((2, chunks, pair_k, ROWS, n), BF),
            pltpu.VMEM((chunks, own_k, ROWS // 2, n), BF),
            pltpu.VMEM((chunks, own_k, ROWS // 2, n), BF),
            pltpu.VMEM((chunks, pair_k, ROWS, n), BF),
            pltpu.VMEM((chunks, pair_k, ROWS, n), BF),
            pltpu.VMEM((chunks, momenta, ROWS, n), BF),
            pltpu.VMEM((nq, n, n), BF),
            pltpu.VMEM((n // height, n, deep), BF),
            pltpu.VMEM((momenta, height, n), BF),
            pltpu.VMEM((momenta + 1, 16, n), F32),
            pltpu.VMEM((nq, pair_k * height, n), BF),
            pltpu.VMEM((pair_k, deep, n), BF),
            pltpu.VMEM((own_k, n, n), BF),
            pltpu.VMEM((own_k, n, n), BF),
            dma((chunks,)), dma(()), dma((len(RELAYED),)), dma((len(RELAYED), chunks)),
            dma((own_k,)), dma((own_k,)), dma((own_k, 2)),
        ],
        compiler_params=pltpu.CompilerParams(
            collective_id=0, has_side_effects=True, vmem_limit_bytes=67_043_328),
        name="scba",
    )(perm, ends, weight, green_blocks, coupling)


def solution(mesh):
    placed = (P("mom", "en", None, None, None), P("mom", None), P("mom"), P(), P())
    return jax.shard_map(
        body,
        mesh=mesh,
        in_specs=placed,
        out_specs=P("mom", "en", None, None, None),
        check_vma=False,
    )
```

profile of v0, /device:TPU:1, one launch (start us, length us, event | category | flops | bytes accessed | tf_op | source)
XLA Modules:
  0.0 217.4 jit_solution(17533838340715472190)
XLA Ops:
  0.0 0.7 copy.13
  0.7 0.8 pad_add_fusion
  1.5 2.0 collective-permute-start
  3.5 0.8 fusion
  4.9 0.0 collective-permute-done
  5.0 0.1 copy.14
  5.1 0.1 copy.18
  5.2 0.1 copy.16
  5.3 0.3 convert_reduce_fusion
  5.5 0.7 select_reduce_fusion.perm
  6.2 0.2 convert_reduce_fusion.1
  6.5 0.7 copy.19.ends
  7.1 0.1 select_select_fusion.3
  7.2 0.7 pad_maximum_fusion.weight
  7.9 202.6 %scba.1 = f32[3,1,2,512,512]{4,3,2,1,0:T(8,128)} custom-call(s32[6,24]{1,0:T(8,128)} %select_reduce_fusion.perm, s32[6,10]{1,0:T(8,128)} %copy.19.ends, f32[6,4]{1,0:T(8,128)} %pad_maximum_fusion.weight, f32[3,1,2,512,512]{4,3,2,1,0:T(8,128)} %green.1, bf16[9,512,512]{2,1,0:T(8,128)(2,1)} %coupling.1), custom_call_target="tpu_custom_call" | custom-call | tf_op jit(solution)/shard_map/scba/pallas_call | solution.py:326
  210.5 6.9 %copy.22 = f32[3,1,2,512,512]{4,3,2,1,0:T(8,128)} copy(f32[3,1,2,512,512]{4,3,2,1,0:T(8,128)} %scba.1) | data formatting | bytes 12582912
  (7 shorter events, 0.1 us)
Async XLA Ops:
  1.5 3.4 %collective-permute-start = (s32[3,25]{1,0:T(4,128)S(1)}, s32[3,25]{1,0:T(4,128)S(1)}, u32[]{:S(2)}, u32[]{:S(2)}) collective-permute-start(s32[3,25]{1,0:T(4,128)S(1)} %pad_add_fusion), channel_id=1, source_target_pairs={{0,64},{16,80},{32,96},{48,112},{64,0},{80,16},{96,32},{112,48},{1... | collective-permute-start | bytes 908 | tf_op jit(solution)/shard_map/ppermute | solution.py:302
where the time goes:
time: 221 us; the launch traced here: 217 us
  Pallas kernels  203 us (92%)
  local copies, waits for them, and re-layouts  8.59 us (4%)
  other arithmetic  3.47 us (2%)
    pallas_call x1, Pallas kernels, body(): pl.pallas_call(functools.partial(kernel, n, nq, own_k), out_shape=jax.Sha...  203 us
    unnamed x1, local copies, waits for them, and re-layouts  6.88 us
  transfers between devices with their start and end apart: 1, of which 0 were waited for; matrix products, arithmetic and copies ran while one was open for 0% of the time, Pallas kernels for 0%

commit v1 on v0

v1 whole, which is shorter than its diff:
```python
import functools

import jax
import jax.numpy as jnp
from jax import lax
from jax.experimental import pallas as pl
from jax.experimental.pallas import tpu as pltpu
from jax.sharding import PartitionSpec as P

MESH = pl.DeviceIdType.MESH
BF = jnp.bfloat16
F32 = jnp.float32

NX, NY, NZ = 2, 4, 4
ROWS = 32
SUB = 2
KSTEP = 3
QSTEP = 3
RELAYED = ("b1", "b3", "a1", "a3", "r1", "r3", "z", "do", "ds", "y1", "yx", "yf", "t0", "t1", "t2", "t3")


def kernel(n, nq, own_k, count, packed, occupancy, green, coupling, out,
           stage, a, own, far, rp, rc, po, ps, whole, cmat, cst, block, prefix, bins, right, tables, order,
           perm, ends, shifts,
           load_sem, cload_sem, send_sem, recv_sem, osend_sem, orecv_sem, table_send, table_recv, table_sem):
    chunks = n // ROWS
    half = ROWS // 2
    height = ROWS * SUB
    blocks = chunks // SUB
    pair_k = 2 * own_k
    every_k = NY * pair_k
    mom, en = lax.axis_index("mom"), lax.axis_index("en")
    xl, y = mom // NY, mom % NY
    z, xh, core = en // 4, (en // 2) % 2, en % 2
    part = xl
    mine, other = xl * own_k, (1 - xl) * own_k
    near, across = y + 1 - 2 * (y % 2), NY - 1 - y
    hub = core == y // 2
    helper = core != y // 2

    def place(axl, ay, az, axh, acore):
        return (axl * NY + ay, (az * 2 + axh) * 2 + acore)

    pair = place(1 - xl, y, z, xh, core)
    cross = place(1 - xl, y, z, 1 - xh, core)
    z_to = place(xl, y, (z + 1 + 2 * xh) % NZ, xh, core)
    z_from = place(xl, y, (z + 3 + 2 * xh) % NZ, xh, core)
    twin = place(xl, y, z, xh, 1 - core)
    y_near = place(xl, near, z, xh, core)
    y_across = place(xl, across, z, xh, core)
    corner = place(1 - xl, across, z, xh, core)
    o_across = place(xl, across, z, xh, 1 - core)
    o_corner = place(1 - xl, across, z, xh, 1 - core)
    side = (core + xh) % 2

    kinds = {name: i for i, name in enumerate(RELAYED)}

    def remote(name, r, src, dst, device):
        i = kinds[name]
        return pltpu.make_async_remote_copy(
            src_ref=src, dst_ref=dst, send_sem=send_sem.at[i], recv_sem=recv_sem.at[i, r],
            device_id=device, device_id_type=MESH)

    def first(r):
        return own.at[r, pl.ds(mine, own_k), pl.ds(0, half)]

    def second(r):
        return own.at[r, pl.ds(mine, own_k), pl.ds(half, half)]

    def copy(name, r):
        if name == "b1":
            return remote(name, r, first(r), rp.at[r], pair)
        if name == "b3":
            return remote(name, r, second(r), rc.at[r], cross)
        if name == "a1":
            return remote(name, r, a.at[r], own.at[r, pl.ds(mine, own_k)], pair)
        if name == "a3":
            return remote(name, r, a.at[r], far.at[0, r, pl.ds(mine, own_k)], cross)
        if name == "r3":
            return remote(name, r, rp.at[r], far.at[0, r, pl.ds(other, own_k), pl.ds(0, half)], cross)
        if name == "r1":
            return remote(name, r, rc.at[r], far.at[0, r, pl.ds(other, own_k), pl.ds(half, half)], pair)
        if name == "z":
            return remote(name, r, far.at[0, r], far.at[1, r], z_to)
        if name == "do":
            return remote(name, r, own.at[r], po.at[r], twin)
        if name == "ds":
            return remote(name, r, far.at[side, r], ps.at[r], twin)

        def group(g):
            return whole.at[r, pl.ds(g * pair_k, pair_k)]

        if name == "y1":
            return remote(name, r, group(y), group(y), y_near)
        if name == "yx":
            return remote(name, r, group(NY), group(y), y_across)
        if name == "yf":
            return remote(name, r, group(across), group(across), y_near)
        g = {"t0": y, "t1": near, "t2": across, "t3": NY - 1 - near}[name]
        return remote(name, r, group(g), group(g), twin)

    def load(r):
        return pltpu.make_async_copy(
            green.at[:, 0, :, pl.ds(r * ROWS, ROWS)], stage.at[:, :, pl.ds(r * ROWS, ROWS)], load_sem.at[r])

    def convert(r):
        rows = pl.ds(r * ROWS, ROWS)
        for j in range(own_k):
            a[r, j] = stage[j, 1 - part, rows].astype(BF)
            own[r, mine + j] = stage[j, part, rows].astype(BF)

    pl.loop(0, chunks)(lambda r: load(r).start())
    cload = pltpu.make_async_copy(coupling, cmat, cload_sem)
    cload.start()
    barrier = pltpu.get_barrier_semaphore()
    everyone = (pair, cross, z_to, z_from, twin, y_near, y_across, corner, o_across, o_corner)
    for device in everyone:
        pl.semaphore_signal(barrier, inc=1, device_id=device, device_id_type=MESH)

    @pl.loop(0, 2)
    def _(r):
        load(r).wait()
        convert(r)

    pl.semaphore_wait(barrier, len(everyone))

    def x_start(r):
        for name in ("b1", "b3", "a1", "a3"):
            copy(name, r).start()

    x_start(0)

    def table_copy(i, device, where):
        return pltpu.make_async_remote_copy(
            src_ref=packed, dst_ref=tables.at[where], send_sem=table_send.at[i], recv_sem=table_recv.at[i],
            device_id=device, device_id_type=MESH)

    sent_tables = [table_copy(0, pair, xl), table_copy(1, y_across, 2 + xl), table_copy(2, corner, 2 + xl)]
    for sent in sent_tables:
        sent.start()
    tables[xl] = packed[...]

    @pl.loop(2, chunks)
    def _(r):
        load(r).wait()
        convert(r)

    def sort_tables():
        for sent in sent_tables:
            sent.wait()
        lane = lax.broadcasted_iota(jnp.int32, (8, 128), 1)
        real = lane < every_k
        first_of = jnp.where(hub, 0, 2)
        slots = [c % (NY * own_k) // own_k * pair_k + c // (NY * own_k) * own_k + c % own_k for c in range(every_k)]
        slot = jnp.zeros((8, 128), jnp.int32)
        for c in range(every_k):
            slot = jnp.where(lane == c, slots[c], slot)
        for g in range(2):
            table = tables[first_of + g]
            key = table * 64 + slot
            rank = jnp.zeros((8, 128), jnp.int32)
            bound = jnp.zeros((8, 128), jnp.int32)
            for c in range(every_k):
                rank += jnp.where(key[:, c:c + 1] < key, 1, 0)
                bound += jnp.where(table[:, c:c + 1] < lane, 1, 0)
            place_of = jnp.zeros((8, 128), jnp.int32)
            for c in range(every_k):
                place_of += jnp.where((rank[:, c:c + 1] == lane) & real, slots[c], 0)
            order[g] = place_of
            order[2 + g] = bound
        copies = [
            pltpu.make_async_copy(order.at[pl.ds(0, 2)], perm, table_sem.at[0]),
            pltpu.make_async_copy(order.at[pl.ds(2, 2)], ends, table_sem.at[1]),
            pltpu.make_async_copy(tables.at[pl.ds(0, 2)], shifts, table_sem.at[2])]
        for c in copies:
            c.start()
        for c in copies:
            c.wait()

    low_occupancy = occupancy[0]
    high_occupancy = low_occupancy + 1.0

    def weights(i):
        shift = shifts[i // own_k, i % own_k, every_k]
        below1 = jnp.where((shift == 1) & (en >= 1), low_occupancy, 0.0)
        above1 = jnp.where((shift == 1) & (en + 1 < count), high_occupancy, 0.0)
        below2 = jnp.where((shift != 1) & (en >= 2), low_occupancy, 0.0)
        above2 = jnp.where((shift != 1) & (en + 2 < count), high_occupancy, 0.0)
        return (jnp.where(core == 0, above1, below1), jnp.where(core == 0, below1, above1),
                jnp.where(xh == 0, above2, below2), jnp.where(xh == 0, below2, above2))

    def mix(r):
        to = jnp.where(hub, y, NY) * pair_k
        for i in range(pair_k):
            w = weights(i)
            total = w[0] * po[r, i].astype(F32)
            total += w[1] * ps[r, i].astype(F32)
            total += w[2] * far[0, r, i].astype(F32)
            total += w[3] * far[1, r, i].astype(F32)
            whole[r, to + i] = total.astype(BF)

    total_of = stage
    tiles = height // 16

    def term(b, k):
        product = jnp.dot(cst[b], right[k], preferred_element_type=F32)
        total_of[k // 2, k % 2] = jnp.where(b == 0, product, total_of[k // 2, k % 2] + product)

    def bin_tile(k, tile):
        rows = pl.ds(tile * 16, 16)
        total = jnp.zeros((16, n), F32)
        for j in range(every_k):
            total += block[perm[k // own_k, k % own_k, j], rows].astype(F32)
            prefix[tile, j + 1] = total
        low = prefix[tile, ends[k // own_k, k % own_k, 0]]
        to = pl.ds(pl.multiple_of((k * tiles + tile) * 16, 16), 16)
        for q in range(nq):
            high = prefix[tile, ends[k // own_k, k % own_k, q + 1]]
            bins[q, to] = (high - low).astype(BF)
            low = high

    def classes(b):
        @pl.loop(0, every_k)
        def _(s):
            for u in range(SUB):
                block[s, u * ROWS:(u + 1) * ROWS] = whole[b * SUB + u, s]

        @pl.loop(0, pair_k, step=KSTEP)
        def _(k0):
            for k in range(KSTEP):
                term(b - 1, k0 + k)
                for tile in range(tiles):
                    bin_tile(k0 + k, tile)

    def classes0():
        @pl.loop(0, every_k)
        def _(s):
            for u in range(SUB):
                block[s, u * ROWS:(u + 1) * ROWS] = whole[u, s]

        @pl.loop(0, pair_k)
        def _(k):
            for tile in range(tiles):
                bin_tile(k, tile)

    def rights():
        @pl.loop(0, nq, step=QSTEP)
        def _(q0):
            for d in range(QSTEP):
                q = q0 + d
                product = lax.dot_general(
                    bins[q], cmat[q], (((1,), (1,)), ((), ())), preferred_element_type=F32).astype(BF)
                at = pl.ds(pl.multiple_of(q * height, height), height)
                for k in range(pair_k):
                    right[k, at] = product[k * height:(k + 1) * height]

    def osend(k, device):
        return pltpu.make_async_remote_copy(
            src_ref=own.at[:, k], dst_ref=out.at[k % own_k, part], send_sem=osend_sem.at[k],
            recv_sem=orecv_sem.at[mine + k % own_k], device_id=device, device_id_type=MESH)

    def keep(k):
        return pltpu.make_async_copy(own.at[:, k], out.at[k % own_k, part], osend_sem.at[k])

    def send_out(k):
        far_side = (k // own_k) != xl

        @pl.when(hub & jnp.logical_not(far_side))
        def _():
            keep(k).start()

        @pl.when(hub & far_side)
        def _():
            osend(k, pair).start()

        @pl.when(helper & far_side)
        def _():
            osend(k, o_corner).start()

        @pl.when(helper & jnp.logical_not(far_side))
        def _():
            osend(k, o_across).start()

    def all_sent(name, ref):
        pltpu.make_async_copy(ref, ref, send_sem.at[kinds[name]]).wait()

    def finish():
        for name, ref in (("b1", rp), ("b3", rc), ("do", own)):
            all_sent(name, ref)

        @pl.loop(0, pair_k)
        def _(i):
            k = (other + i) % pair_k
            product = jnp.dot(cst[blocks - 1], right[k], preferred_element_type=F32)
            product = (total_of[k // 2, k % 2] + product) * (1.0 / every_k)
            own[:, k] = product.astype(BF).reshape(chunks, ROWS, n)

            @pl.when(i >= 1)
            def _():
                send_out((other + i - 1) % pair_k)

        send_out((other + pair_k - 1) % pair_k)

    def within(r):
        return (r >= 0) & (r < chunks)

    @pl.loop(0, chunks + 6)
    def _(t):
        @pl.when(within(t))
        def _():
            copy("b1", t).wait_recv()
            copy("r3", t).start()
            copy("b3", t).wait_recv()
            copy("r1", t).start()

        @pl.when(within(t + 1))
        def _():
            x_start(t + 1)

        @pl.when(t == 0)
        def _():
            cload.wait()
            prefix[:, 0] = jnp.zeros((tiles, 16, n), F32)
            right[:, nq * height:] = jnp.zeros((pair_k, right.shape[1] - nq * height, n), BF)
            lane = lax.broadcasted_iota(jnp.int32, (n, 128), 1) < height

            @pl.loop(0, (nq + 1) // 2)
            def _(h):
                for d in range(n // 128):
                    lhs = cmat[2 * h, :, d * 128:(d + 1) * 128].astype(F32)
                    rhs = cmat[jnp.minimum(2 * h + 1, nq - 1), :, d * 128:(d + 1) * 128].astype(F32)
                    rhs = jnp.where(2 * h + 1 < nq, rhs, jnp.zeros_like(rhs))
                    to = pl.ds(pl.multiple_of(h * 128, 128), 128)
                    cst[2 * d, :, to] = jnp.where(lane, lhs, pltpu.roll(rhs, height, 1)).astype(BF)
                    cst[2 * d + 1, :, to] = jnp.where(lane, pltpu.roll(lhs, height, 1), rhs).astype(BF)

        @pl.when(t == 1)
        def _():
            sort_tables()

        @pl.when(within(t - 1))
        def _():
            r = t - 1
            copy("a3", r).wait_recv()
            copy("r3", r).wait_recv()
            copy("r1", r).wait_recv()
            copy("z", r).start()
            copy("a1", r).wait_recv()
            copy("do", r).start()

        @pl.when(within(t - 2))
        def _():
            r = t - 2
            copy("z", r).wait_recv()
            copy("ds", r).start()

        @pl.when(within(t - 5))
        def _():
            r = t - 5

            @pl.when(helper)
            def _():
                for name in ("t0", "t2", "t1", "t3"):
                    copy(name, r).wait_recv()

            @pl.when(r == SUB - 1)
            def _():
                classes0()

            @pl.when((r % SUB == SUB - 1) & (r >= SUB))
            def _():
                classes(r // SUB)

        @pl.when(within(t - 6) & ((t - 6) % SUB == SUB - 1))
        def _():
            rights()

        @pl.when(within(t - 3) & hub)
        def _():
            r = t - 3
            copy("yx", r).wait_recv()
            copy("yf", r).start()
            copy("t2", r).start()

        @pl.when(within(t - 4) & hub)
        def _():
            r = t - 4
            copy("y1", r).wait_recv()
            copy("t1", r).start()
            copy("yf", r).wait_recv()
            copy("t3", r).start()

        @pl.when(within(t - 2))
        def _():
            r = t - 2
            copy("do", r).wait_recv()
            copy("ds", r).wait_recv()
            mix(r)

        @pl.when(within(t - 2) & hub)
        def _():
            copy("y1", t - 2).start()
            copy("t0", t - 2).start()

        @pl.when(within(t - 2) & helper)
        def _():
            copy("yx", t - 2).start()

    finish()

    for name, ref in (("a1", a), ("a3", a), ("r1", rc), ("r3", rp), ("z", far.at[0]), ("ds", ps)):
        all_sent(name, ref)

    @pl.when(hub)
    def _():
        for name in ("y1", "yf", "t0", "t1", "t2", "t3"):
            all_sent(name, ps)

    @pl.when(helper)
    def _():
        all_sent("yx", ps)

    for k in range(pair_k):
        mine_too = hub & ((k // own_k) == xl)

        @pl.when(mine_too)
        def _():
            keep(k).wait()

        @pl.when(jnp.logical_not(mine_too))
        def _():
            osend(k, pair).wait_send()
    for p in range(2):
        for j in range(own_k):
            @pl.when(helper | (p != xl))
            def _():
                pltpu.make_async_copy(out.at[j, p], out.at[j, p], orecv_sem.at[p * own_k + j]).wait()


def body(green_blocks, transfer_index, photon_shift, photon_occupancy, coupling):
    own_k, n = green_blocks.shape[0], green_blocks.shape[3]
    momenta, nq = transfer_index.shape[1], coupling.shape[0]
    pair_k = 2 * own_k
    chunks, height = n // ROWS, ROWS * SUB
    deep = (nq + 1) // 2 * 2 * height
    count = lax.axis_size("en")
    packed = jnp.concatenate([transfer_index, photon_shift[:, None]], axis=1)
    packed = jnp.pad(packed, ((0, 8 - own_k), (0, 128 - momenta - 1)))

    smem = pl.BlockSpec(memory_space=pltpu.SMEM)
    hbm = pl.BlockSpec(memory_space=pl.ANY)
    dma = pltpu.SemaphoreType.DMA
    parts = pl.pallas_call(
        functools.partial(kernel, n, nq, own_k, count),
        out_shape=jax.ShapeDtypeStruct((own_k, 2, chunks, ROWS, n), BF),
        in_specs=[pl.BlockSpec(memory_space=pltpu.VMEM), smem, hbm, hbm],
        out_specs=hbm,
        scratch_shapes=[
            pltpu.VMEM((own_k, 2, n, n), F32),
            pltpu.VMEM((chunks, own_k, ROWS, n), BF),
            pltpu.VMEM((chunks, pair_k, ROWS, n), BF),
            pltpu.VMEM((2, chunks, pair_k, ROWS, n), BF),
            pltpu.VMEM((chunks, own_k, ROWS // 2, n), BF),
            pltpu.VMEM((chunks, own_k, ROWS // 2, n), BF),
            pltpu.VMEM((chunks, pair_k, ROWS, n), BF),
            pltpu.VMEM((chunks, pair_k, ROWS, n), BF),
            pltpu.VMEM((chunks, momenta + pair_k, ROWS, n), BF),
            pltpu.VMEM((nq, n, n), BF),
            pltpu.VMEM((n // height, n, deep), BF),
            pltpu.VMEM((momenta, height, n), BF),
            pltpu.VMEM((height // 16, momenta + 1, 16, n), F32),
            pltpu.VMEM((nq, pair_k * height, n), BF),
            pltpu.VMEM((pair_k, deep, n), BF),
            pltpu.VMEM((4, 8, 128), jnp.int32),
            pltpu.VMEM((4, 8, 128), jnp.int32),
            pltpu.SMEM((2, 8, 128), jnp.int32),
            pltpu.SMEM((2, 8, 128), jnp.int32),
            pltpu.SMEM((2, 8, 128), jnp.int32),
            dma((chunks,)), dma(()), dma((len(RELAYED),)), dma((len(RELAYED), chunks)),
            dma((pair_k,)), dma((pair_k,)), dma((3,)), dma((3,)), dma((3,)),
        ],
        compiler_params=pltpu.CompilerParams(
            collective_id=0, has_side_effects=True, vmem_limit_bytes=67_043_328),
        name="scba",
    )(packed, photon_occupancy, green_blocks, coupling)
    return parts.reshape(green_blocks.shape).astype(F32)


def solution(mesh):
    placed = (P("mom", "en", None, None, None), P("mom", None), P("mom"), P(), P())
    return jax.shard_map(
        body,
        mesh=mesh,
        in_specs=placed,
        out_specs=P("mom", "en", None, None, None),
        check_vma=False,
    )
```

time: 221 us -> 170 us (0.77); the launches traced: 217 us -> 169 us
  Pallas kernels: 203 us -> 161 us
  local copies, waits for them, and re-layouts: 8.59 us -> 1.34 us
  other arithmetic: 3.47 us -> 6.22 us
    pallas_call x1, Pallas kernels: 203 us -> 161 us  [body(): pl.pallas_call(functools.partial(kernel, n, nq, own_k, count), out_shape=...]
    unnamed x1 -> x0, local copies, waits for them, and re-layouts: 6.88 us -> none
    convert_element_type x0 -> x1, other arithmetic: none -> 5.47 us  [body(): return parts.reshape(green_blocks.shape).astype(F32)]
  transfers between devices with their start and end apart: 1 -> 0, of which waited for: 0 -> 0; matrix products, arithmetic and copies ran while one was open for 0% -> 0% of each run, Pallas kernels for 0% -> 0%
where the time goes in v1:
time: 170 us; the launch traced here: 169 us
  Pallas kernels  161 us (95%)
  other arithmetic  6.22 us (4%)
    pallas_call x1, Pallas kernels, body(): pl.pallas_call(functools.partial(kernel, n, nq, own_k, count), out_shape=...  161 us
    convert_element_type x1, other arithmetic, body(): return parts.reshape(green_blocks.shape).astype(F32)  5.47 us

profile of v1, /device:TPU:1, one launch (start us, length us, event | category | flops | bytes accessed | tf_op | source)
XLA Modules:
  0.0 169.5 jit_solution(7221122993595762583)
XLA Ops:
  0.7 0.7 copy.6
  1.4 0.8 pad_add_fusion
  2.1 0.6 pad.4.packed
  2.7 161.2 %scba.1 = bf16[3,2,16,32,512]{4,3,2,1,0:T(8,128)(2,1)} custom-call(s32[8,128]{1,0:T(8,128)} %pad.4.packed, f32[1]{0:T(128)S(6)} %copy.8.occupancy, f32[3,1,2,512,512]{4,3,2,1,0:T(8,128)} %green.1, bf16[9,512,512]{2,1,0:T(8,128)(2,1)} %coupling.1), custom_call_target="tpu_custom_call" | custom-call | tf_op jit(solution)/shard_map/scba/pallas_call | solution.py:453
  164.0 5.5 %convert.2 = f32[3,1,2,512,512]{4,3,2,1,0:T(8,128)} convert(bf16[3,1,2,512,512]{4,3,2,1,0:T(8,128)(2,1)} %bitcast.6) | non-fusion elementwise | flops 1572864 | bytes 9437184 | tf_op jit(solution)/shard_map/convert_element_type | solution.py:486

commit v2 on v1

--- a/solution.py
+++ b/solution.py
@@ -24,7 +24,7 @@
            perm, ends, shifts,
            load_sem, cload_sem, send_sem, recv_sem, osend_sem, orecv_sem, table_send, table_recv, table_sem):
     chunks = n // ROWS
-    half = ROWS // 2
+    half = n // 2
     height = ROWS * SUB
     blocks = chunks // SUB
     pair_k = 2 * own_k
@@ -62,10 +62,10 @@
             device_id=device, device_id_type=MESH)
 
     def first(r):
-        return own.at[r, pl.ds(mine, own_k), pl.ds(0, half)]
+        return own.at[r, pl.ds(mine, own_k), :, pl.ds(0, half)]
 
     def second(r):
-        return own.at[r, pl.ds(mine, own_k), pl.ds(half, half)]
+        return own.at[r, pl.ds(mine, own_k), :, pl.ds(half, half)]
 
     def copy(name, r):
         if name == "b1":
@@ -77,9 +77,9 @@
         if name == "a3":
             return remote(name, r, a.at[r], far.at[0, r, pl.ds(mine, own_k)], cross)
         if name == "r3":
-            return remote(name, r, rp.at[r], far.at[0, r, pl.ds(other, own_k), pl.ds(0, half)], cross)
+            return remote(name, r, rp.at[r], far.at[0, r, pl.ds(other, own_k), :, pl.ds(0, half)], cross)
         if name == "r1":
-            return remote(name, r, rc.at[r], far.at[0, r, pl.ds(other, own_k), pl.ds(half, half)], pair)
+            return remote(name, r, rc.at[r], far.at[0, r, pl.ds(other, own_k), :, pl.ds(half, half)], pair)
         if name == "z":
             return remote(name, r, far.at[0, r], far.at[1, r], z_to)
         if name == "do":
@@ -219,25 +219,19 @@
             bins[q, to] = (high - low).astype(BF)
             low = high
 
-    def classes(b):
+    def take(b):
         @pl.loop(0, every_k)
         def _(s):
             for u in range(SUB):
                 block[s, u * ROWS:(u + 1) * ROWS] = whole[b * SUB + u, s]
 
-        @pl.loop(0, pair_k, step=KSTEP)
-        def _(k0):
-            for k in range(KSTEP):
-                term(b - 1, k0 + k)
-                for tile in range(tiles):
-                    bin_tile(k0 + k, tile)
+    def classes(b, k0):
+        for k in range(k0, k0 + own_k):
+            term(b - 1, k)
+            for tile in range(tiles):
+                bin_tile(k, tile)
 
     def classes0():
-        @pl.loop(0, every_k)
-        def _(s):
-            for u in range(SUB):
-                block[s, u * ROWS:(u + 1) * ROWS] = whole[u, s]
-
         @pl.loop(0, pair_k)
         def _(k):
             for tile in range(tiles):
@@ -304,8 +298,24 @@
     def within(r):
         return (r >= 0) & (r < chunks)
 
-    @pl.loop(0, chunks + 6)
+    @pl.loop(0, chunks + 8)
     def _(t):
+        @pl.when(within(t - 4))
+        def _():
+            r = t - 4
+            copy("do", r).wait_recv()
+            copy("ds", r).wait_recv()
+            mix(r)
+
+        @pl.when(within(t - 4) & hub)
+        def _():
+            copy("y1", t - 4).start()
+            copy("t0", t - 4).start()
+
+        @pl.when(within(t - 4) & helper)
+        def _():
+            copy("yx", t - 4).start()
+
         @pl.when(within(t))
         def _():
             copy("b1", t).wait_recv()
@@ -348,63 +358,52 @@
             copy("a1", r).wait_recv()
             copy("do", r).start()
 
-        @pl.when(within(t - 2))
-        def _():
-            r = t - 2
+        @pl.when(within(t - 3))
+        def _():
+            r = t - 3
             copy("z", r).wait_recv()
             copy("ds", r).start()
 
-        @pl.when(within(t - 5))
-        def _():
-            r = t - 5
+        @pl.when(within(t - 7))
+        def _():
+            r = t - 7
 
             @pl.when(helper)
             def _():
                 for name in ("t0", "t2", "t1", "t3"):
                     copy(name, r).wait_recv()
 
+            @pl.when(r % SUB == SUB - 1)
+            def _():
+                take(r // SUB)
+
             @pl.when(r == SUB - 1)
             def _():
                 classes0()
 
             @pl.when((r % SUB == SUB - 1) & (r >= SUB))
             def _():
-                classes(r // SUB)
-
-        @pl.when(within(t - 6) & ((t - 6) % SUB == SUB - 1))
+                classes(r // SUB, 0)
+                classes(r // SUB, own_k)
+
+        @pl.when(within(t - 8) & ((t - 8) % SUB == SUB - 1))
         def _():
             rights()
 
-        @pl.when(within(t - 3) & hub)
-        def _():
-            r = t - 3
+        @pl.when(within(t - 5) & hub)
+        def _():
+            r = t - 5
             copy("yx", r).wait_recv()
             copy("yf", r).start()
             copy("t2", r).start()
 
-        @pl.when(within(t - 4) & hub)
-        def _():
-            r = t - 4
+        @pl.when(within(t - 6) & hub)
+        def _():
+            r = t - 6
             copy("y1", r).wait_recv()
             copy("t1", r).start()
             copy("yf", r).wait_recv()
             copy("t3", r).start()
-
-        @pl.when(within(t - 2))
-        def _():
-            r = t - 2
-            copy("do", r).wait_recv()
-            copy("ds", r).wait_recv()
-            mix(r)
-
-        @pl.when(within(t - 2) & hub)
-        def _():
-            copy("y1", t - 2).start()
-            copy("t0", t - 2).start()
-
-        @pl.when(within(t - 2) & helper)
-        def _():
-            copy("yx", t - 2).start()
 
     finish()
 
@@ -460,8 +459,8 @@
             pltpu.VMEM((chunks, own_k, ROWS, n), BF),
             pltpu.VMEM((chunks, pair_k, ROWS, n), BF),
             pltpu.VMEM((2, chunks, pair_k, ROWS, n), BF),
-            pltpu.VMEM((chunks, own_k, ROWS // 2, n), BF),
-            pltpu.VMEM((chunks, own_k, ROWS // 2, n), BF),
+            pltpu.VMEM((chunks, own_k, ROWS, n // 2), BF),
+            pltpu.VMEM((chunks, own_k, ROWS, n // 2), BF),
             pltpu.VMEM((chunks, pair_k, ROWS, n), BF),
             pltpu.VMEM((chunks, pair_k, ROWS, n), BF),
             pltpu.VMEM((chunks, momenta + pair_k, ROWS, n), BF),

time: 170 us -> 163 us (0.959)
  Pallas kernels: 161 us -> 154 us
    pallas_call x1, Pallas kernels: 161 us -> 154 us  [body(): pl.pallas_call(functools.partial(kernel, n, nq, own_k, count), out_shape=...]
where the time goes in v2:
time: 163 us; the launch traced here: 162 us
  Pallas kernels  154 us (94%)
  other arithmetic  6.22 us (4%)
    pallas_call x1, Pallas kernels, body(): pl.pallas_call(functools.partial(kernel, n, nq, own_k, count), out_shape=...  154 us
    convert_element_type x1, other arithmetic, body(): return parts.reshape(green_blocks.shape).astype(F32)  5.47 us

profile of v2, /device:TPU:1, one launch (start us, length us, event | category | flops | bytes accessed | tf_op | source)
XLA Modules:
  0.0 162.5 jit_solution(5379798068882616801)
XLA Ops:
  0.7 0.7 copy.6
  1.4 0.8 pad_add_fusion
  2.1 0.6 pad.4.packed
  2.7 154.3 %scba.1 = bf16[3,2,16,32,512]{4,3,2,1,0:T(8,128)(2,1)} custom-call(s32[8,128]{1,0:T(8,128)} %pad.4.packed, f32[1]{0:T(128)S(6)} %copy.8.occupancy, f32[3,1,2,512,512]{4,3,2,1,0:T(8,128)} %green.1, bf16[9,512,512]{2,1,0:T(8,128)(2,1)} %coupling.1), custom_call_target="tpu_custom_call" | custom-call | tf_op jit(solution)/shard_map/scba/pallas_call | solution.py:452
  157.0 5.5 %convert.2 = f32[3,1,2,512,512]{4,3,2,1,0:T(8,128)} convert(bf16[3,1,2,512,512]{4,3,2,1,0:T(8,128)(2,1)} %bitcast.6) | non-fusion elementwise | flops 1572864 | bytes 9437184 | tf_op jit(solution)/shard_map/convert_element_type | solution.py:485

commit v3 on v2

--- a/solution.py
+++ b/solution.py
@@ -19,8 +19,8 @@
 RELAYED = ("b1", "b3", "a1", "a3", "r1", "r3", "z", "do", "ds", "y1", "yx", "yf", "t0", "t1", "t2", "t3")
 
 
-def kernel(n, nq, own_k, count, packed, occupancy, green, coupling, out,
-           stage, a, own, far, rp, rc, po, ps, whole, cmat, cst, block, prefix, bins, right, tables, order,
+def kernel(n, nq, own_k, count, classes_in, shift_in, occupancy, green, coupling, out,
+           stage, a, own, far, rp, rc, po, ps, whole, cmat, cst, block, prefix, bins, right, packed, tables, order,
            perm, ends, shifts,
            load_sem, cload_sem, send_sem, recv_sem, osend_sem, orecv_sem, table_send, table_recv, table_sem):
     chunks = n // ROWS
@@ -112,6 +112,13 @@
     pl.loop(0, chunks)(lambda r: load(r).start())
     cload = pltpu.make_async_copy(coupling, cmat, cload_sem)
     cload.start()
+    row8 = lax.broadcasted_iota(jnp.int32, (8, 128), 0)
+    lane8 = lax.broadcasted_iota(jnp.int32, (8, 128), 1)
+    shifted = jnp.zeros((8, 128), jnp.int32)
+    for j in range(own_k):
+        shifted = jnp.where((row8 == j) & (lane8 == every_k), shift_in[j], shifted)
+    packed[...] = shifted
+    packed[0:own_k, 0:every_k] = classes_in[...]
     barrier = pltpu.get_barrier_semaphore()
     everyone = (pair, cross, z_to, z_from, twin, y_near, y_across, corner, o_across, o_corner)
     for device in everyone:
@@ -129,6 +136,7 @@
             copy(name, r).start()
 
     x_start(0)
+    x_start(1)
 
     def table_copy(i, device, where):
         return pltpu.make_async_remote_copy(
@@ -323,9 +331,9 @@
             copy("b3", t).wait_recv()
             copy("r1", t).start()
 
-        @pl.when(within(t + 1))
-        def _():
-            x_start(t + 1)
+        @pl.when(within(t + 2))
+        def _():
+            x_start(t + 2)
 
         @pl.when(t == 0)
         def _():
@@ -443,16 +451,13 @@
     chunks, height = n // ROWS, ROWS * SUB
     deep = (nq + 1) // 2 * 2 * height
     count = lax.axis_size("en")
-    packed = jnp.concatenate([transfer_index, photon_shift[:, None]], axis=1)
-    packed = jnp.pad(packed, ((0, 8 - own_k), (0, 128 - momenta - 1)))
-
     smem = pl.BlockSpec(memory_space=pltpu.SMEM)
     hbm = pl.BlockSpec(memory_space=pl.ANY)
     dma = pltpu.SemaphoreType.DMA
     parts = pl.pallas_call(
         functools.partial(kernel, n, nq, own_k, count),
         out_shape=jax.ShapeDtypeStruct((own_k, 2, chunks, ROWS, n), BF),
-        in_specs=[pl.BlockSpec(memory_space=pltpu.VMEM), smem, hbm, hbm],
+        in_specs=[pl.BlockSpec(memory_space=pltpu.VMEM), smem, smem, hbm, hbm],
         out_specs=hbm,
         scratch_shapes=[
             pltpu.VMEM((own_k, 2, n, n), F32),
@@ -470,6 +475,7 @@
             pltpu.VMEM((height // 16, momenta + 1, 16, n), F32),
             pltpu.VMEM((nq, pair_k * height, n), BF),
             pltpu.VMEM((pair_k, deep, n), BF),
+            pltpu.VMEM((8, 128), jnp.int32),
             pltpu.VMEM((4, 8, 128), jnp.int32),
             pltpu.VMEM((4, 8, 128), jnp.int32),
             pltpu.SMEM((2, 8, 128), jnp.int32),
@@ -481,7 +487,7 @@
         compiler_params=pltpu.CompilerParams(
             collective_id=0, has_side_effects=True, vmem_limit_bytes=67_043_328),
         name="scba",
-    )(packed, photon_occupancy, green_blocks, coupling)
+    )(transfer_index, photon_shift, photon_occupancy, green_blocks, coupling)
     return parts.reshape(green_blocks.shape).astype(F32)
 
 

time: 163 us -> 161 us (0.988)
  no operation moved by 1% of the time
where the time goes in v3:
time: 161 us; the launch traced here: 160 us
  Pallas kernels  154 us (96%)
  other arithmetic  5.47 us (3%)
    pallas_call x1, Pallas kernels, body(): pl.pallas_call(functools.partial(kernel, n, nq, own_k, count), out_shape=...  154 us
    convert_element_type x1, other arithmetic, body(): return parts.reshape(green_blocks.shape).astype(F32)  5.47 us

profile of v3, /device:TPU:1, one launch (start us, length us, event | category | flops | bytes accessed | tf_op | source)
XLA Modules:
  0.0 160.4 jit_solution(3383558992391827625)
XLA Ops:
  0.7 154.3 %scba.1 = bf16[3,2,16,32,512]{4,3,2,1,0:T(8,128)(2,1)} custom-call(s32[3,24]{1,0:T(4,128)} %classes_in.1, s32[3]{0:T(128)} %shift_in.1, f32[1]{0:T(128)S(6)} %copy.7.occupancy, f32[3,1,2,512,512]{4,3,2,1,0:T(8,128)} %green.1, bf16[9,512,512]{2,1,0:T(8,128)(2,1)} %coupling.1), custom_call_target="tpu_custom_call" | custom-call | tf_op jit(solution)/shard_map/scba/pallas_call | solution.py:457
  154.9 5.5 %convert.2 = f32[3,1,2,512,512]{4,3,2,1,0:T(8,128)} convert(bf16[3,1,2,512,512]{4,3,2,1,0:T(8,128)(2,1)} %bitcast.5) | non-fusion elementwise | flops 1572864 | bytes 9437184 | tf_op jit(solution)/shard_map/convert_element_type | solution.py:491
